TPU v7x, 512 devices: a whole 4x8x8 slice. The times are simulated.
512 devices in a mesh: blk: 32 (over z, y_lo), head: 16 (over x, y_hi, core).
Axes of the slice: x: 4, y: 8 (y_hi: 2, y_lo: 4; y = y_hi * 4 + y_lo), z: 8, core: 2. Of those that a mesh axis runs over, the one named last changes fastest.
Arguments:
- queries: bfloat16 [16384, 1024], P('blk', 'head'), may hold values from -170 to 170
- key_rows: bfloat16 [16384, 1024], P('blk', 'head'), may hold values from -9 to 9
- values: bfloat16 [16384, 1024], P('blk', 'head'), may hold values from -48 to 48
- text_keys: bfloat16 [1232, 1024], P(None, 'head'), may hold values from -9 to 9
- text_values: bfloat16 [1232, 1024], P(None, 'head'), may hold values from -48 to 48
- block_image: int32 [128], replicated, may hold values from 0 to 7, as said below
- gate_image: float32 [8, 1536], replicated, may hold values from 0.5 to 2
- residual: bfloat16 [16384, 1536], P(('blk', 'head')), may hold values from -6 to 6
- w_out: bfloat16 [1024, 1536], P('head'), may hold values from -0.1875 to 0.1875
Outputs:
- stream_out: bfloat16 [16384, 1536], P(('blk', 'head'))
Inputs may be any that keep to these rules, and one draw needn't show every extreme that they name: `block_image`: each image number 0 to 7 names 8 to 24 of the entries, some image exactly 24 and some exactly 8; the blocks of an image lie anywhere in the array.
All inputs are finite; a program needn't handle non-finite values.
Results may differ from a plain program's by a relative error of at most 0.014.
Values may be sent and summed in bfloat16 or wider, within the bound.
A program may use at most 64 MiB of HBM per device.

v0:
```python
import math
import jax
import jax.numpy as jnp
from jax import lax
from jax.sharding import PartitionSpec as P

HD = 64
TEXT = 154
BS = 128
neg_large = -1e30


def side_by_side(arrays, axis, dim, along):
    widths = [a.shape[along] for a in arrays]
    both = jnp.concatenate(arrays, axis=along)
    result = lax.all_gather(both, axis, axis=dim, tiled=True)
    return tuple(jnp.split(result, [sum(widths[:k]) for k in range(1, len(widths))], axis=along))


def absorb(running, query_three, query_image, key_slab, value_slab, key_image):
    best, total, accum = running
    heads = query_three.shape[1]
    width = query_three.shape[2]
    key_three = key_slab.reshape(key_slab.shape[0], heads, width)
    value_three = value_slab.reshape(value_slab.shape[0], heads, width)
    scores = jnp.einsum("qhd,khd->hqk", query_three, key_three, preferred_element_type=jnp.float32)
    scores = scores * (1.0 / math.sqrt(width))
    allowed = query_image[:, None] == key_image[None, :]
    scores = jnp.where(allowed[None], scores, neg_large)
    newbest = jnp.maximum(best, jnp.max(scores, axis=2))
    weights = jnp.exp(scores - newbest[..., None])
    shrink = jnp.exp(best - newbest)
    total = total * shrink + jnp.sum(weights, axis=2)
    update = jnp.einsum(
        "hqk,khd->hqd",
        weights.astype(jnp.bfloat16),
        value_three,
        preferred_element_type=jnp.float32,
    )
    accum = accum * shrink[..., None] + update
    return (newbest, total, accum)


def on_device(
    queries, key_rows, values, text_keys, text_values, block_image, gate_image, residual, w_out
):
    tok_blk = queries.shape[0]
    ncols = queries.shape[1]
    heads_here = ncols // HD
    blocks_here = tok_blk // BS
    token_image = jnp.repeat(block_image, BS)
    blk_index = lax.axis_index("blk")
    my_blocks = lax.dynamic_slice_in_dim(block_image, blk_index * blocks_here, blocks_here)
    query_image = jnp.repeat(my_blocks, BS)
    text_image = jnp.arange(text_keys.shape[0]) // TEXT
    start_state = (
        jnp.full((heads_here, tok_blk), neg_large, jnp.float32),
        jnp.zeros((heads_here, tok_blk), jnp.float32),
        jnp.zeros((heads_here, tok_blk, HD), jnp.float32),
    )
    query_three = queries.reshape(tok_blk, heads_here, HD)
    running = absorb(start_state, query_three, query_image, text_keys, text_values, text_image)
    fold_running = running
    key_piece, value_piece = side_by_side((key_rows, values), "blk", 0, 1)
    length = key_piece.shape[0]

    def advance(state, position):
        begin = position * tok_blk
        key_slab = lax.dynamic_slice_in_dim(key_piece, begin, tok_blk)
        value_slab = lax.dynamic_slice_in_dim(value_piece, begin, tok_blk)
        slab_image = lax.dynamic_slice_in_dim(token_image, begin, tok_blk)
        return (absorb(state, query_three, query_image, key_slab, value_slab, slab_image), None)

    fold_running, unused = lax.scan(
        advance, fold_running, jnp.arange(length // tok_blk, dtype=jnp.int32)
    )
    best, total, accum = fold_running
    attended = (accum / total[..., None]).astype(jnp.bfloat16)
    attended = attended.transpose(1, 0, 2).reshape(tok_blk, ncols)
    tok_dev = tok_blk // lax.axis_size("head")
    mixed = lax.all_to_all(attended, "head", split_axis=0, concat_axis=1, tiled=True)
    projected = jnp.dot(
        mixed, lax.all_gather(w_out, "head", axis=0, tiled=True), preferred_element_type=jnp.float32
    )
    head_index = lax.axis_index("head")
    row_image = lax.dynamic_slice_in_dim(query_image, head_index * tok_dev, tok_dev)
    onehot = (
        row_image[:, None] == jnp.arange(gate_image.shape[0], dtype=jnp.int32)[None, :]
    ).astype(jnp.float32)
    gating = jnp.dot(onehot, gate_image, precision=lax.Precision.HIGHEST)
    return (residual.astype(jnp.float32) + gating * projected).astype(jnp.bfloat16)


def solution(mesh):
    placed = (
        P("blk", "head"),
        P("blk", "head"),
        P("blk", "head"),
        P(None, "head"),
        P(None, "head"),
        P(),
        P(),
        P(("blk", "head"), None),
        P("head", None),
    )
    return jax.shard_map(
        on_device, mesh=mesh, in_specs=placed, out_specs=P(("blk", "head"), None), check_vma=False
    )
```

profile of v0, /device:TPU:1, one launch (start us, length us, event | category | flops | bytes accessed | tf_op | source)
XLA Modules:
  0.0 353.7 jit_solution(8619565113360705211)
XLA Ops:
  11.6 1.5 fusion.35
  14.2 148.3 %all-gather.3.cloned.1.call-done = bf16[16384,128]{1,0:T(8,128)(2,1)} async-done(((bf16[512,128]{1,0:T(8,128)(2,1)}), bf16[16384,128]{1,0:T(8,128)(2,1)}) %all-gather.3.cloned.1.call-update) | async-done | bytes 4194320 | tf_op jit(solution)/shard_map/all_gather | solution.py:16
  162.5 7.3 %fusion.34 = (bf16[16384,64]{1,0:T(8,128)(2,1)}, bf16[16384,64]{1,0:T(8,128)(2,1)}) fusion(bf16[16384,128]{1,0:T(8,128)(2,1)} %all-gather.3.cloned.1.call-done), kind=kLoop, calls=%fused_computation.48 | loop fusion | bytes 8388608 | tf_op jit(solution)/shard_map/split | solution.py:17
  169.9 133.4 %while.15 = (s32[]{:T(128)}, f32[1,512]{1,0:T(1,128)S(1)}, f32[1,512]{1,0:T(1,128)S(1)}, f32[1,512,64]{1,2,0:T(8,128)S(1)}, s32[32]{0:T(128)S(1)}, /*index=5*/s3...) while((s32[]{:T(128)}, f32[1,512]{1,0:T(1,128)S(1)}, ...), condition=%wide.region_5.6_spmd.clone, body=%wide.region_2.5_spmd.clone.sunk | while | flops 69272576 | bytes 3778779 | solution.py:74
  172.8 1.2 fusion.51
  175.5 1.2 fusion.49
  176.9 1.2 fusion.51
  181.1 1.2 fusion.51
  185.3 1.2 fusion.51
  189.4 1.2 fusion.51
  192.2 1.2 fusion.49
  193.6 1.2 fusion.51
  197.8 1.2 fusion.51
  201.9 1.2 fusion.51
  206.1 1.2 fusion.51
  210.3 1.2 fusion.51
  214.4 1.2 fusion.51
  218.6 1.2 fusion.51
  221.3 1.2 fusion.49
  222.8 1.2 fusion.51
  226.9 1.2 fusion.51
  231.1 1.2 fusion.51
  235.3 1.2 fusion.51
  239.4 1.2 fusion.51
  242.2 1.2 fusion.49
  243.6 1.2 fusion.51
  246.3 1.2 fusion.49
  247.8 1.2 fusion.51
  250.5 1.2 fusion.49
  252.0 1.3 fusion.51
  254.7 1.2 fusion.49
  256.2 1.2 fusion.51
  260.3 1.2 fusion.51
  264.5 1.2 fusion.51
  268.7 1.2 fusion.51
  271.4 1.2 fusion.49
  272.8 1.2 fusion.51
  277.0 1.2 fusion.51
  281.2 1.2 fusion.51
  285.3 1.2 fusion.51
  288.1 1.2 fusion.49
  289.5 1.2 fusion.51
  293.7 1.2 fusion.51
  297.8 1.2 fusion.51
  302.0 1.2 fusion.51
  304.3 29.3 %all-to-all-start = ((bf16[16,2,1024]{2,1,0:T(2,128)(2,1)}), bf16[16,2,1024]{2,1,0:T(2,128)(2,1)S(1)}, u32[]{:S(2)}, u32[]{:S(2)}) async-start(bf16[16,2,1024]{2,1,0:T(2,128)(2,1)} %reshape.134), calls=%async_computation | async-start | bytes 131072 | tf_op jit(solution)/shard_map/all_to_all | solution.py:81
  333.8 9.4 %all-to-all-done = bf16[16,2,1024]{2,1,0:T(2,128)(2,1)S(1)} async-done(((bf16[16,2,1024]{2,1,0:T(2,128)(2,1)}), bf16[16,2,1024]{2,1,0:T(2,128)(2,1)S(1)}, u32[]{:S(2)}, u32[]{:S(2)}) %all-to-all-start) | async-done | bytes 65568 | tf_op jit(solution)/shard_map/all_to_all | solution.py:81
  343.7 3.2 fusion.16
  (282 shorter events, 67.9 us)
Async XLA Ops:
  6.5 5.1 %copy-start = (bf16[1232,64]{0,1:T(8,128)(2,1)S(1)}, bf16[1232,64]{0,1:T(8,128)(2,1)}, u32[]{:S(2)}) copy-start(bf16[1232,64]{0,1:T(8,128)(2,1)} %param.14) | copy-start | bytes 473092
  6.5 155.9 %all-gather.3.cloned.1.call-start = ((), (), s32[]{:S(2)}) async-start(), calls=%async_computation.1 | async-start | bytes 4325376 | tf_op jit(solution)/shard_map/all_gather | solution.py:16
  9.3 334.4 %all-gather.5.cloned.1.call-start = ((), (), s32[]{:S(2)}) async-start(), calls=%async_computation.2 | async-start | bytes 3342336 | tf_op jit(solution)/shard_map/all_gather | solution.py:83
  11.6 2.0 copy-start.1
  14.2 155.6 %copy-start.4 = (bf16[512,64]{0,1:T(8,128)(2,1)S(1)}, bf16[512,64]{0,1:T(8,128)(2,1)}, u32[]{:S(2)}) copy-start(bf16[512,64]{0,1:T(8,128)(2,1)} %param.11) | copy-start | bytes 196612
  169.8 163.7 %copy-start.3 = (f32[8,1536]{1,0:T(8,128)S(1)}, f32[8,1536]{1,0:T(8,128)}, u32[]{:S(2)}) copy-start(f32[8,1536]{1,0:T(8,128)} %param.17) | copy-start | bytes 147460
  169.8 173.8 %copy-start.2 = (bf16[32,1536]{1,0:T(8,128)(2,1)S(1)}, bf16[32,1536]{1,0:T(8,128)(2,1)}, u32[]{:S(2)}) copy-start(bf16[32,1536]{1,0:T(8,128)(2,1)} %param.18) | copy-start | bytes 294916
  304.3 39.0 %all-to-all-start = ((bf16[16,2,1024]{2,1,0:T(2,128)(2,1)}), bf16[16,2,1024]{2,1,0:T(2,128)(2,1)S(1)}, u32[]{:S(2)}, u32[]{:S(2)}) async-start(bf16[16,2,1024]{2,1,0:T(2,128)(2,1)} %reshape.134), calls=%async_computation | async-start | bytes 131072 | tf_op jit(solution)/shard_map/all_to_all | solution.py:81
Sparse Core Ops, SparseCore 0:
  9.4 153.0 all-gather.2
  165.8 94.2 all-gather.4
where the time goes:
time: 355 us; the launch traced here: 354 us
  waiting for transfers between devices  158 us (45%)
  matrix products  83 us (23%)
  local copies, waits for them, and re-layouts  37.7 us (11%)
  starting transfers between devices  29.3 us (8%)
  loops' own time  23.2 us (7%)
  between operations  13.5 us (4%)
  other arithmetic  8.42 us (2%)
    all_gather x1, waiting for transfers between devices, side_by_side(): result = lax.all_gather(both, axis, axis=dim, tiled=True)  148 us
    dot_general x33, matrix products, absorb(): jnp.einsum('qhd,khd->hqk', query_three, key_three, preferred_element_type...  39.8 us
    dot_general x33, matrix products, absorb(): jnp.einsum('hqk,khd->hqd', weights.astype(jnp.bfloat16), value_three, pre...  39.7 us
    all_to_all x1, starting transfers between devices, on_device(): lax.all_to_all(attended, 'head', split_axis=0, concat_axis=1, tiled=True)  29.3 us
    another operation x1, loops' own time, on_device(): lax.scan(advance, fold_running, jnp.arange(length // tok_blk, dtype=jnp.i...  23.2 us
    dynamic_slice x32, local copies, waits for them, and re-layouts, on_device(): lax.scan(advance, fold_running, jnp.arange(length // tok_blk, dtype=jnp.i...  20.8 us
    all_to_all x1, waiting for transfers between devices, on_device(): lax.all_to_all(attended, 'head', split_axis=0, concat_axis=1, tiled=True)  9.44 us
    split x1, local copies, waits for them, and re-layouts, side_by_side(): jnp.split(result, [sum(widths[:k]) for k in range(1, len(widths))], axis=...  7.34 us
  transfers between devices with their start and end apart: 3, of which 2 were waited for; matrix products, arithmetic and copies ran while one was open for 35% of the time, Pallas kernels for 0%

commit v1 on v0

--- a/solution.py
+++ b/solution.py
@@ -78,7 +78,10 @@
     attended = (accum / total[..., None]).astype(jnp.bfloat16)
     attended = attended.transpose(1, 0, 2).reshape(tok_blk, ncols)
     tok_dev = tok_blk // lax.axis_size("head")
-    mixed = lax.all_to_all(attended, "head", split_axis=0, concat_axis=1, tiled=True)
+    mixed = jnp.concatenate(
+        lax.all_to_all(jnp.stack(jnp.split(attended, lax.axis_size("head"), axis=0)), "head", 0, 0),
+        axis=1,
+    )
     projected = jnp.dot(
         mixed, lax.all_gather(w_out, "head", axis=0, tiled=True), preferred_element_type=jnp.float32
     )

time: 355 us -> 356 us (level)
  no operation moved by 1% of the time
where the time goes in v1:
time: 356 us; the launch traced here: 354 us
  waiting for transfers between devices  158 us (44%)
  matrix products  83 us (23%)
  local copies, waits for them, and re-layouts  37.9 us (11%)
  starting transfers between devices  29.3 us (8%)
  loops' own time  23.2 us (7%)
  between operations  13.6 us (4%)
  other arithmetic  8.42 us (2%)
    all_gather x1, waiting for transfers between devices, side_by_side(): result = lax.all_gather(both, axis, axis=dim, tiled=True)  148 us
    dot_general x33, matrix products, absorb(): jnp.einsum('qhd,khd->hqk', query_three, key_three, preferred_element_type...  39.8 us
    dot_general x33, matrix products, absorb(): jnp.einsum('hqk,khd->hqd', weights.astype(jnp.bfloat16), value_three, pre...  39.7 us
    all_to_all x1, starting transfers between devices, on_device(): lax.all_to_all(jnp.stack(jnp.split(attended, lax.axis_size('head'), axis=...  29.3 us
    another operation x1, loops' own time, on_device(): lax.scan(advance, fold_running, jnp.arange(length // tok_blk, dtype=jnp.i...  23.2 us
    dynamic_slice x32, local copies, waits for them, and re-layouts, on_device(): lax.scan(advance, fold_running, jnp.arange(length // tok_blk, dtype=jnp.i...  20.8 us
    all_to_all x1, waiting for transfers between devices, on_device(): lax.all_to_all(jnp.stack(jnp.split(attended, lax.axis_size('head'), axis=...  9.44 us
    split x1, local copies, waits for them, and re-layouts, side_by_side(): jnp.split(result, [sum(widths[:k]) for k in range(1, len(widths))], axis=...  7.34 us
  transfers between devices with their start and end apart: 3, of which 2 were waited for; matrix products, arithmetic and copies ran while one was open for 35% of the time, Pallas kernels for 0%

profile of v1, /device:TPU:1, one launch (start us, length us, event | category | flops | bytes accessed | tf_op | source)
XLA Modules:
  0.0 353.9 jit_solution(5157665660335921528)
XLA Ops:
  11.6 1.5 fusion.35
  14.2 148.3 %all-gather.3.cloned.1.call-done = bf16[16384,128]{1,0:T(8,128)(2,1)} async-done(((bf16[512,128]{1,0:T(8,128)(2,1)}), bf16[16384,128]{1,0:T(8,128)(2,1)}) %all-gather.3.cloned.1.call-update) | async-done | bytes 4194320 | tf_op jit(solution)/shard_map/all_gather | solution.py:16
  162.5 7.3 %fusion.34 = (bf16[16384,64]{1,0:T(8,128)(2,1)}, bf16[16384,64]{1,0:T(8,128)(2,1)}) fusion(bf16[16384,128]{1,0:T(8,128)(2,1)} %all-gather.3.cloned.1.call-done), kind=kLoop, calls=%fused_computation.64 | loop fusion | bytes 8388608 | tf_op jit(solution)/shard_map/split | solution.py:17
  169.9 133.4 %while.15 = (s32[]{:T(128)}, f32[1,512]{1,0:T(1,128)S(1)}, f32[1,512]{1,0:T(1,128)S(1)}, f32[1,512,64]{1,2,0:T(8,128)S(1)}, s32[32]{0:T(128)S(1)}, /*index=5*/s3...) while((s32[]{:T(128)}, f32[1,512]{1,0:T(1,128)S(1)}, ...), condition=%wide.region_5.6_spmd.clone, body=%wide.region_2.5_spmd.clone.sunk | while | flops 69272576 | bytes 3778779 | solution.py:74
  172.8 1.2 fusion.51
  175.5 1.2 fusion.49
  176.9 1.2 fusion.51
  181.1 1.2 fusion.51
  185.3 1.2 fusion.51
  189.4 1.2 fusion.51
  192.2 1.2 fusion.49
  193.6 1.2 fusion.51
  197.8 1.2 fusion.51
  201.9 1.2 fusion.51
  206.1 1.2 fusion.51
  210.3 1.2 fusion.51
  214.4 1.2 fusion.51
  218.6 1.2 fusion.51
  221.3 1.2 fusion.49
  222.8 1.2 fusion.51
  226.9 1.2 fusion.51
  231.1 1.2 fusion.51
  235.3 1.2 fusion.51
  239.4 1.2 fusion.51
  242.2 1.2 fusion.49
  243.6 1.2 fusion.51
  246.3 1.2 fusion.49
  247.8 1.2 fusion.51
  250.5 1.2 fusion.49
  252.0 1.3 fusion.51
  254.7 1.2 fusion.49
  256.2 1.2 fusion.51
  260.3 1.2 fusion.51
  264.5 1.2 fusion.51
  268.7 1.2 fusion.51
  271.4 1.2 fusion.49
  272.8 1.2 fusion.51
  277.0 1.2 fusion.51
  281.2 1.2 fusion.51
  285.3 1.2 fusion.51
  288.1 1.2 fusion.49
  289.5 1.2 fusion.51
  293.7 1.2 fusion.51
  297.8 1.2 fusion.51
  302.0 1.2 fusion.51
  304.5 29.3 %all-to-all-start = ((bf16[16,2,1024]{2,1,0:T(2,128)(2,1)}), bf16[16,2,1024]{2,1,0:T(2,128)(2,1)S(1)}, u32[]{:S(2)}, u32[]{:S(2)}) async-start(bf16[16,2,1024]{2,1,0:T(2,128)(2,1)} %reshape.170), calls=%async_computation | async-start | bytes 131072 | tf_op jit(solution)/shard_map/all_to_all | solution.py:82
  334.0 9.4 %all-to-all-done = bf16[16,2,1024]{2,1,0:T(2,128)(2,1)S(1)} async-done(((bf16[16,2,1024]{2,1,0:T(2,128)(2,1)}), bf16[16,2,1024]{2,1,0:T(2,128)(2,1)S(1)}, u32[]{:S(2)}, u32[]{:S(2)}) %all-to-all-start) | async-done | bytes 65568 | tf_op jit(solution)/shard_map/all_to_all | solution.py:82
  343.9 3.2 fusion.16
  (298 shorter events, 68.0 us)
Async XLA Ops:
  6.5 5.1 %copy-start = (bf16[1232,64]{0,1:T(8,128)(2,1)S(1)}, bf16[1232,64]{0,1:T(8,128)(2,1)}, u32[]{:S(2)}) copy-start(bf16[1232,64]{0,1:T(8,128)(2,1)} %param.14) | copy-start | bytes 473092
  6.5 155.9 %all-gather.3.cloned.1.call-start = ((), (), s32[]{:S(2)}) async-start(), calls=%async_computation.1 | async-start | bytes 4325376 | tf_op jit(solution)/shard_map/all_gather | solution.py:16
  9.3 334.5 %all-gather.5.cloned.1.call-start = ((), (), s32[]{:S(2)}) async-start(), calls=%async_computation.2 | async-start | bytes 3342336 | tf_op jit(solution)/shard_map/all_gather | solution.py:86
  11.6 2.0 copy-start.1
  14.2 155.6 %copy-start.4 = (bf16[512,64]{0,1:T(8,128)(2,1)S(1)}, bf16[512,64]{0,1:T(8,128)(2,1)}, u32[]{:S(2)}) copy-start(bf16[512,64]{0,1:T(8,128)(2,1)} %param.11) | copy-start | bytes 196612
  169.8 163.9 %copy-start.3 = (f32[8,1536]{1,0:T(8,128)S(1)}, f32[8,1536]{1,0:T(8,128)}, u32[]{:S(2)}) copy-start(f32[8,1536]{1,0:T(8,128)} %param.17) | copy-start | bytes 147460
  169.8 174.0 %copy-start.2 = (bf16[32,1536]{1,0:T(8,128)(2,1)S(1)}, bf16[32,1536]{1,0:T(8,128)(2,1)}, u32[]{:S(2)}) copy-start(bf16[32,1536]{1,0:T(8,128)(2,1)} %param.18) | copy-start | bytes 294916
  304.5 39.0 %all-to-all-start = ((bf16[16,2,1024]{2,1,0:T(2,128)(2,1)}), bf16[16,2,1024]{2,1,0:T(2,128)(2,1)S(1)}, u32[]{:S(2)}, u32[]{:S(2)}) async-start(bf16[16,2,1024]{2,1,0:T(2,128)(2,1)} %reshape.170), calls=%async_computation | async-start | bytes 131072 | tf_op jit(solution)/shard_map/all_to_all | solution.py:82
Sparse Core Ops, SparseCore 0:
  9.4 153.0 all-gather.2
  165.8 94.2 all-gather.4
